TPU v7x, 256 devices: a whole 4x4x8 slice. The times are simulated.
256 devices in a mesh: rep: 2 (over y_lo), shard: 128 (over z, x, y_hi, core).
Axes of the slice: x: 4, y: 4 (y_hi: 2, y_lo: 2; y = y_hi * 2 + y_lo), z: 8, core: 2. Of those that a mesh axis runs over, the one named last changes fastest.
Arguments:
- row_ids: int32 [2, 128, 128, 16], P('rep', 'shard'), may hold values from -1 to 1310719, as said below
- grad_rows: bfloat16 [2, 128, 128, 16, 128], P('rep', 'shard'), may hold values from -6 to 6
- touched: int32 [128, 20], P('shard'), may hold values from 0 to 39, as said below
- block_home: int32 [5120], replicated, may hold values from 0 to 5119, as said below
- embed_table: float32 [1310720, 128], P('shard'), may hold values from -4 to 4
- row_accum: float32 [1310720], P('shard'), may hold values from 0.001 to 0.1
Outputs:
- new_table: float32 [1310720, 128], P('shard')
- new_accum: float32 [1310720], P('shard')
Inputs may be any that keep to these rules, and one draw needn't show every extreme that they name: block_home is a permutation of 0 to 5119. Each row of touched holds 20 different local block numbers. `row_ids`: A live slot in bucket d of any device names a logical row whose stored row lies on index d of shard, in a local block listed in row d of touched; about three quarters of the slots are live.
All inputs are finite; a program needn't handle non-finite values.
Results may differ from a plain program's by a relative error of at most 0.0003.
Values may be sent and summed in bfloat16 or wider, within the bound.
A program may use at most 64 MiB of HBM per device.

v0:
```python
import functools
import math

import jax
import jax.numpy as jnp
from jax import lax
from jax.sharding import Mesh
from jax.sharding import PartitionSpec as P

BLOCK = 256
SHARD = ("shard_0", "shard_1", "shard_2", "shard_3")


CLIP_RMS = 0.25
LEARN_RATE = 0.1
DECAY_RATE = 0.05


def sent_to_all(x, axis):
    copies = jnp.broadcast_to(x, (lax.axis_size(axis), *x.shape))
    return lax.all_to_all(copies, axis, split_axis=0, concat_axis=0, tiled=True)


def in_order(parts, dim):
    parts = jnp.moveaxis(parts, 0, dim)
    shape = parts.shape
    return parts.reshape(*shape[:dim], shape[dim] * shape[dim + 1], *shape[dim + 2 :])


def gather_directly(x, axis, dim):
    parts = sent_to_all(x, axis)
    return in_order(parts, dim)


def over_axes(x, axes):
    return functools.reduce(lax.psum, axes, x)


def block_sums(slot_keys, gradients, touch_count):
    offsets = lax.broadcasted_iota(jnp.int32, (BLOCK, 1), 0)

    def single_block(slot_index):
        onehot = (slot_keys[None, :] == slot_index * BLOCK + offsets).astype(jnp.bfloat16)
        return jnp.dot(onehot, gradients, preferred_element_type=jnp.float32)

    return lax.map(single_block, jnp.arange(touch_count, dtype=jnp.int32))


def adagrad(old_rows, old_accum, gradient):
    next_accum = old_accum + jnp.mean(gradient * gradient, axis=-1)
    next_rows = (
        old_rows * (1.0 - DECAY_RATE) - LEARN_RATE * gradient / jnp.sqrt(next_accum)[..., None]
    )
    return (next_rows, next_accum)


def slot_blocks(recv_ids, recv_grads, block_home, listed, blocks_here, feature_width):
    sample_ids = recv_ids.reshape(-1)
    gradients = recv_grads.reshape(-1, feature_width)
    is_live = sample_ids >= 0
    safe_ids = jnp.where(is_live, sample_ids, 0)
    local_block = block_home[safe_ids // BLOCK] % blocks_here
    touch_count = listed.shape[0]
    matches = local_block[:, None] == listed[None, :]
    positions = jnp.arange(touch_count, dtype=jnp.int32)[None, :]
    slot_index = jnp.sum(jnp.where(matches, positions, 0), axis=1)
    located = jnp.any(matches, axis=1) & is_live
    slot_keys = jnp.where(located, slot_index * BLOCK + safe_ids % BLOCK, -1)
    return block_sums(slot_keys, gradients, touch_count)


def body(row_ids, grad_rows, touched, block_home, embed_table, row_accum):
    feature_width = grad_rows.shape[-1]
    recv_ids, recv_grads = (
        lax.all_to_all(row_ids, SHARD, split_axis=2, concat_axis=2, tiled=True),
        lax.all_to_all(grad_rows, SHARD, split_axis=2, concat_axis=2, tiled=True),
    )
    recv_ids, recv_grads = (
        gather_directly(recv_ids, "rep", 0),
        gather_directly(recv_grads, "rep", 0),
    )
    blocks_here = embed_table.shape[0] // BLOCK
    listed = touched[0]
    touch_count = listed.shape[0]
    blocks = slot_blocks(recv_ids, recv_grads, block_home, listed, blocks_here, feature_width)
    table_blocks = embed_table.reshape(blocks_here, BLOCK, feature_width)
    accum_blocks = row_accum.reshape(blocks_here, BLOCK)
    entries = lax.axis_size(SHARD) * touch_count * BLOCK * feature_width
    clip_limit = CLIP_RMS * math.sqrt(entries)
    old_rows = table_blocks[listed]
    old_accum = accum_blocks[listed]
    square_sum = over_axes(jnp.sum(blocks * blocks), SHARD)
    clip_factor = clip_limit / jnp.maximum(jnp.sqrt(square_sum), clip_limit)
    new_rows, new_accum = adagrad(old_rows, old_accum, blocks * clip_factor)
    table_out = table_blocks.at[listed].set(new_rows).reshape(-1, feature_width)
    accum_out = accum_blocks.at[listed].set(new_accum).reshape(-1)
    return (table_out, accum_out)


def solution(mesh):
    split = Mesh(
        mesh.devices.reshape(mesh.shape["rep"], 8, 4, 2, 2),
        ("rep", "shard_0", "shard_1", "shard_2", "shard_3"),
    )
    placed = (
        P("rep", SHARD, None, None),
        P("rep", SHARD, None, None, None),
        P(SHARD, None),
        P(),
        P(SHARD, None),
        P(SHARD),
    )
    return jax.shard_map(
        body, mesh=split, in_specs=placed, out_specs=(P(SHARD, None), P(SHARD)), check_vma=False
    )
```

profile of v0, /device:TPU:1, one launch (start us, length us, event | category | flops | bytes accessed | tf_op | source)
XLA Modules:
  0.0 216.2 jit_solution(14793037254866139673)
XLA Ops:
  0.7 4.3 %copy.32 = f32[10240,128]{1,0:T(8,128)} copy(f32[10240,128]{1,0:T(8,128)} %param.12) | data formatting | bytes 10485760
  4.9 0.7 copy.15
  5.7 16.4 %all-to-all-start = ((s32[1,1,128,16]{3,1,0,2:T(1,128)}), s32[1,1,128,16]{3,1,0,2:T(1,128)S(1)}, u32[]{:S(2)}, u32[]{:S(2)}) async-start(s32[1,1,128,16]{3,1,0,2:T(1,128)} %copy.15), calls=%async_computation | async-start | bytes 131072 | tf_op jit(solution)/shard_map/all_to_all | solution.py:75
  22.1 11.7 %all-to-all-done = s32[1,1,128,16]{3,1,0,2:T(1,128)S(1)} async-done(((s32[1,1,128,16]{3,1,0,2:T(1,128)}), s32[1,1,128,16]{3,1,0,2:T(1,128)S(1)}, u32[]{:S(2)}, u32[]{:S(2)}) %all-to-all-start) | async-done | bytes 8224 | tf_op jit(solution)/shard_map/all_to_all | solution.py:75
  33.9 0.6 broadcast_in_dim.40
  34.5 3.2 %all-to-all-start.1 = ((s32[2,1,1,128,16]{3,4,2,1,0:T(8,128)}), s32[2,1,1,128,16]{3,4,2,1,0:T(8,128)S(1)}, u32[]{:S(2)}, u32[]{:S(2)}) async-start(s32[2,1,1,128,16]{3,4,2,1,0:T(8,128)} %broadcast_in_dim.40), calls=%async_computation.1 | async-start | bytes 32768 | tf_op jit(solution)/shard_map/all_to_all | solution.py:21
  37.8 2.7 %all-to-all-done.1 = s32[2,1,1,128,16]{3,4,2,1,0:T(8,128)S(1)} async-done(((s32[2,1,1,128,16]{3,4,2,1,0:T(8,128)}), s32[2,1,1,128,16]{3,4,2,1,0:T(8,128)S(1)}, u32[]{:S(2)}, u32[]{:S(2)}) %all-to-all-start.1) | async-done | bytes 16416 | tf_op jit(solution)/shard_map/all_to_all | solution.py:21
  40.4 7.4 %all-to-all-start.2 = ((bf16[1,1,128,16,128]{4,3,1,0,2:T(8,128)(2,1)}), bf16[1,1,128,16,128]{4,3,1,0,2:T(8,128)(2,1)S(1)}, u32[]{:S(2)}, u32[]{:S(2)}) async-start(bf16[1,1,128,16,128]{4,3,1,0,2:T(8,128)(2,1)} %bitcast.44), calls=%async_computation.2 | async-start | bytes 1048576 | tf_op jit(solution)/shard_map/all_to_all | solution.py:76
  48.2 23.0 %gather_fusion.1 = s32[4096]{0:T(1024)S(1)} fusion(s32[5120]{0:T(1024)S(1)} %copy-done, s32[4096]{0:T(1024)S(1)} %broadcast_clamp_fusion), kind=kCustom, calls=%fused_computation.1 | custom fusion | bytes 49152 | tf_op jit(solution)/shard_map/gather | solution.py:62
  71.2 1.2 broadcast_in_dim.44
  72.4 4.4 %all-to-all-start.3 = ((bf16[2,1,1,128,16,128]{5,4,3,2,1,0:T(8,128)(2,1)}), bf16[2,1,1,128,16,128]{5,4,3,2,1,0:T(8,128)(2,1)}, u32[]{:S(2)}, u32[]{:S(2)}) async-start(bf16[2,1,1,128,16,128]{5,4,3,2,1,0:T(8,128)(2,1)} %broadcast_in_dim.44), calls=%async_computation.3 | async-start | bytes 2097152 | tf_op jit(solution)/shard_map/all_to_all | solution.py:21
  77.3 12.3 %all-to-all-done.3 = bf16[2,1,1,128,16,128]{5,4,3,2,1,0:T(8,128)(2,1)} async-done(((bf16[2,1,1,128,16,128]{5,4,3,2,1,0:T(8,128)(2,1)}), bf16[2,1,1,128,16,128]{5,4,3,2,1,0:T(8,128)(2,1)}, u32[]{:S(2)}, u32[]{:S(2)}) %all-to-all-start.3) | async-done | bytes 1048608 | tf_op jit(solution)/shard_map/all_to_all | solution.py:21
  89.6 65.1 %while.11 = (s32[]{:T(128)}, f32[20,256,128]{2,1,0:T(8,128)S(1)}, s32[4096]{0:T(1024)S(1)}, s32[20]{0:T(128)S(1)}, bf16[4096,128]{1,0:T(8,128)(2,1)}, /*index=5*/s32[]{:T(128)}, s32[1]{0:T(128)}) while((s32[]{:T(128)}, f32[20,256,128]{2,1,0:T(8,128)S(1)}, s32[4096]{0:T(1024)S(1)}, s32[20]{0:T(128)S(1)}, ...), condition=%wide.region_3.4_spmd.clone, body=%wide.region_2.3_spmd.clone.sunk | while | flops 269484288 | bytes 1198197 | solution.py:46
  89.6 0.6 dynamic_slice.6
  90.8 2.0 fusion.25
  92.9 0.6 dynamic_slice.6
  94.1 2.0 fusion.25
  96.1 0.6 dynamic_slice.6
  97.4 2.0 fusion.25
  99.4 0.6 dynamic_slice.6
  100.6 2.0 fusion.25
  102.6 0.6 dynamic_slice.6
  103.9 2.0 fusion.25
  105.9 0.6 dynamic_slice.6
  107.1 2.0 fusion.25
  109.1 0.6 dynamic_slice.6
  110.4 2.0 fusion.25
  112.4 0.6 dynamic_slice.6
  113.6 2.0 fusion.25
  115.6 0.6 dynamic_slice.6
  116.9 2.0 fusion.25
  118.9 0.6 dynamic_slice.6
  120.2 2.0 fusion.25
  122.2 0.6 dynamic_slice.6
  123.4 2.0 fusion.25
  125.4 0.6 dynamic_slice.6
  126.7 2.0 fusion.25
  128.7 0.6 dynamic_slice.6
  129.9 2.0 fusion.25
  131.9 0.6 dynamic_slice.6
  133.2 2.0 fusion.25
  135.2 0.6 dynamic_slice.6
  136.4 2.0 fusion.25
  138.4 0.6 dynamic_slice.6
  139.7 2.0 fusion.25
  141.7 0.6 dynamic_slice.6
  142.9 2.0 fusion.25
  145.0 0.6 dynamic_slice.6
  146.2 2.0 fusion.25
  148.2 0.6 dynamic_slice.6
  149.5 2.0 fusion.25
  151.5 0.6 dynamic_slice.6
  152.7 2.0 fusion.25
  154.7 1.3 multiply_reduce_fusion.1
  156.0 15.5 %psum.28 = f32[]{:T(128)} all-reduce(f32[]{:T(128)} %multiply_reduce_fusion.1), channel_id=1, replica_groups=mesh['rep'=2,'shard_0'=8,'shard_1'=4,'shard_2'=2,'shard_3'=2] {'shard_0'}, use_global_device_ids=true, to_apply=%region_5.6 | all-reduce | flops 1 | bytes 8 | tf_op jit(solution)/shard_map/psum | solution.py:36
  171.6 9.1 %psum.29 = f32[]{:T(128)} all-reduce(f32[]{:T(128)} %psum.28), channel_id=1, replica_groups=mesh['rep'=2,'shard_0'=8,'shard_1'=4,'shard_2'=2,'shard_3'=2] {'shard_1'}, use_global_device_ids=true, to_apply=%region_6.7 | all-reduce | flops 1 | bytes 8 | tf_op jit(solution)/shard_map/psum | solution.py:36
  181.2 5.9 %psum.30 = f32[]{:T(128)} all-reduce(f32[]{:T(128)} %psum.29), channel_id=1, replica_groups=mesh['rep'=2,'shard_0'=8,'shard_1'=4,'shard_2'=2,'shard_3'=2] {'shard_2'}, use_global_device_ids=true, to_apply=%region_7.8 | all-reduce | flops 1 | bytes 8 | tf_op jit(solution)/shard_map/psum | solution.py:36
  187.1 4.7 %gather_fusion = f32[20,256,128]{2,1,0:T(8,128)} fusion(f32[40,256,128]{2,1,0:T(8,128)} %bitcast.39, s32[1024]{0:T(1024)S(1)} %pad_clamp_fusion), kind=kCustom, calls=%fused_computation | custom fusion | bytes 5242960 | tf_op jit(solution)/shard_map/gather | solution.py:90
  191.8 10.6 %psum.31 = f32[]{:T(128)} all-reduce(f32[]{:T(128)} %psum.30), channel_id=1, replica_groups=mesh['rep'=2,'shard_0'=8,'shard_1'=4,'shard_2'=2,'shard_3'=2] {'shard_3'}, use_global_device_ids=true, to_apply=%region_8.9 | all-reduce | flops 1 | bytes 8 | tf_op jit(solution)/shard_map/psum | solution.py:36
  203.2 0.7 multiply_reduce_fusion
  204.0 0.7 scatter_custom_fusion.1
  204.7 0.6 copy.20
  205.3 3.4 %divide_subtract_fusion = f32[20,256,128]{2,1,0:T(8,128)} fusion(f32[20,256,128]{2,1,0:T(8,128)} %gather_fusion, f32[20,256,128]{2,1,0:T(8,128)S(1)} %get-tuple-element.34, f32[20,256]{1,0:T(8,128)S(1)} %fusion.17, f32[]{:T(128)S(6)} %div.33), kind=kLoop, calls=%fused_computation.13 | loop fusion | flops 3276800 | bytes 7884804 | tf_op jit(solution)/shard_map/sub | solution.py:52
  208.7 7.5 %scatter_fusion = f32[40,256,128]{2,1,0:T(8,128)} fusion(f32[40,256,128]{2,1,0:T(8,128)} %bitcast.40, s32[20]{0:T(128)S(1)} %fusion.18, f32[20,256,128]{2,1,0:T(8,128)} %divide_subtract_fusion), kind=kCustom, calls=%fused_computation.3 | custom fusion | bytes 7864400 | tf_op jit(solution)/shard_map/scatter | solution.py:95
  (46 shorter events, 1.5 us)
Async XLA Ops:
  0.6 47.6 %copy-start = (s32[5120]{0:T(1024)S(1)}, s32[5120]{0:T(1024)}, u32[]{:S(2)}) copy-start(s32[5120]{0:T(1024)} %param.11) | copy-start | bytes 61444
  0.6 4.3 %copy-start.2 = (s32[1,1,128,16]{2,3,1,0:T(8,128)S(1)}, s32[1,1,128,16]{2,3,1,0:T(8,128)}, u32[]{:S(2)}) copy-start(s32[1,1,128,16]{2,3,1,0:T(8,128)} %param.8) | copy-start | bytes 24580
  0.7 21.4 %copy-start.3 = (s32[1,20]{1,0:T(1,128)S(1)}, s32[1,20]{1,0:T(1,128)}, u32[]{:S(2)}) copy-start(s32[1,20]{1,0:T(1,128)} %param.10) | copy-start | bytes 244
  5.7 28.1 %all-to-all-start = ((s32[1,1,128,16]{3,1,0,2:T(1,128)}), s32[1,1,128,16]{3,1,0,2:T(1,128)S(1)}, u32[]{:S(2)}, u32[]{:S(2)}) async-start(s32[1,1,128,16]{3,1,0,2:T(1,128)} %copy.15), calls=%async_computation | async-start | bytes 131072 | tf_op jit(solution)/shard_map/all_to_all | solution.py:75
  34.5 5.9 %all-to-all-start.1 = ((s32[2,1,1,128,16]{3,4,2,1,0:T(8,128)}), s32[2,1,1,128,16]{3,4,2,1,0:T(8,128)S(1)}, u32[]{:S(2)}, u32[]{:S(2)}) async-start(s32[2,1,1,128,16]{3,4,2,1,0:T(8,128)} %broadcast_in_dim.40), calls=%async_computation.1 | async-start | bytes 32768 | tf_op jit(solution)/shard_map/all_to_all | solution.py:21
  40.4 30.8 %all-to-all-start.2 = ((bf16[1,1,128,16,128]{4,3,1,0,2:T(8,128)(2,1)}), bf16[1,1,128,16,128]{4,3,1,0,2:T(8,128)(2,1)S(1)}, u32[]{:S(2)}, u32[]{:S(2)}) async-start(bf16[1,1,128,16,128]{4,3,1,0,2:T(8,128)(2,1)} %bitcast.44), calls=%async_computation.2 | async-start | bytes 1048576 | tf_op jit(solution)/shard_map/all_to_all | solution.py:76
  72.4 17.2 %all-to-all-start.3 = ((bf16[2,1,1,128,16,128]{5,4,3,2,1,0:T(8,128)(2,1)}), bf16[2,1,1,128,16,128]{5,4,3,2,1,0:T(8,128)(2,1)}, u32[]{:S(2)}, u32[]{:S(2)}) async-start(bf16[2,1,1,128,16,128]{5,4,3,2,1,0:T(8,128)(2,1)} %broadcast_in_dim.44), calls=%async_computation.3 | async-start | bytes 2097152 | tf_op jit(solution)/shard_map/all_to_all | solution.py:21
  154.7 1.3 copy-start.1
where the time goes:
time: 218 us; the launch traced here: 216 us
  local copies, waits for them, and re-layouts  55.4 us (25%)
  blocking collectives  41.2 us (19%)
  matrix products  39.7 us (18%)
  starting transfers between devices  31.4 us (14%)
  waiting for transfers between devices  26.7 us (12%)
  loops' own time  13.5 us (6%)
  other arithmetic  6.65 us (3%)
    psum x4, blocking collectives, over_axes(): return functools.reduce(lax.psum, axes, x)  41.2 us
    dot_general x20, matrix products, single_block(): return jnp.dot(onehot, gradients, preferred_element_type=jnp.float32)  39.7 us
    gather x1, local copies, waits for them, and re-layouts, slot_blocks(): local_block = block_home[safe_ids // BLOCK] % blocks_here  23 us
    all_to_all x1, starting transfers between devices, body(): lax.all_to_all(row_ids, SHARD, split_axis=2, concat_axis=2, tiled=True)  16.4 us
    all_to_all x2, waiting for transfers between devices, sent_to_all(): return lax.all_to_all(copies, axis, split_axis=0, concat_axis=0, tiled=True)  15 us
    another operation x1, loops' own time, block_sums(): return lax.map(single_block, jnp.arange(touch_count, dtype=jnp.int32))  13.5 us
    dynamic_slice x20, local copies, waits for them, and re-layouts, block_sums(): return lax.map(single_block, jnp.arange(touch_count, dtype=jnp.int32))  11.7 us
    all_to_all x1, waiting for transfers between devices, body(): lax.all_to_all(row_ids, SHARD, split_axis=2, concat_axis=2, tiled=True)  11.7 us
  transfers between devices with their start and end apart: 4, of which 3 were waited for; matrix products, arithmetic and copies ran while one was open for 11% of the time, Pallas kernels for 0%

commit v1 on v0

v1 whole, which is shorter than its diff:
```python
import functools
import math

import jax
import jax.numpy as jnp
from jax import lax
from jax.experimental import pallas as pl
from jax.experimental.pallas import tpu as pltpu
from jax.sharding import PartitionSpec as P

MESH = pl.DeviceIdType.MESH
BLOCK = 256
PLANE = 16
CLIP_RMS = 0.25
LEARN_RATE = 0.1
DECAY_RATE = 0.05


def key_kernel(blocks_here, ids_ref, home_ref, code_ref):
    ids = ids_ref[...]
    slots, dests = ids.shape
    live = ids >= 0
    safe = jnp.where(live, ids, 0)
    logical = safe >> 8
    high, low = logical >> 7, logical & 127
    stored = jnp.zeros_like(ids)
    for h in range(home_ref.shape[0]):
        row = jnp.broadcast_to(home_ref[h : h + 1, :], ids.shape)
        stored = jnp.where(high == h, jnp.take_along_axis(row, low, axis=1), stored)
    owner = lax.broadcasted_iota(jnp.int32, ids.shape, 1)
    local = stored - owner * blocks_here
    code = jnp.where(live, local * BLOCK + (safe & (BLOCK - 1)), -1)
    padded = jnp.concatenate([code, jnp.zeros((128 - slots, dests), jnp.int32)], axis=0)
    code_ref[...] = padded.T


def exchange_kernel(
    clip_limit,
    grads_hbm,
    codes_ref,
    touched_ref,
    sums_ref,
    clip_ref,
    staged,
    held,
    codes,
    red,
    stage_sem,
    self_sem,
    grad_send,
    grad_recv,
    code_send,
    code_recv,
    pass_send,
    pass_recv,
    passc_send,
    passc_recv,
    red_send,
    red_recv,
):
    rep, me = lax.axis_index("rep"), lax.axis_index("shard")
    shards = held.shape[1]
    planes = shards // PLANE
    z, w = me // PLANE, me % PLANE
    group = (rep + (me // 2) % 2) % 2
    partner = (1 - rep, me)

    def peer_of(d):
        return ((group + (d // 2) % 2) % 2, d)

    stage = pltpu.make_async_copy(grads_hbm, staged, stage_sem)
    stage.start()

    barrier = pltpu.get_barrier_semaphore()
    pl.semaphore_signal(barrier, inc=1, device_id=partner, device_id_type=MESH)

    def greet(i, carry):
        d = (me + i) % shards
        pl.semaphore_signal(barrier, inc=1, device_id=peer_of(d), device_id_type=MESH)
        return carry

    lax.fori_loop(1, shards, greet, 0)
    stage.wait()
    pl.semaphore_wait(barrier, shards)

    def send(d):
        pltpu.make_async_remote_copy(
            src_ref=staged.at[d],
            dst_ref=held.at[group, me],
            send_sem=grad_send,
            recv_sem=grad_recv.at[z],
            device_id=peer_of(d),
            device_id_type=MESH,
        ).start()
        pltpu.make_async_remote_copy(
            src_ref=codes_ref.at[d],
            dst_ref=codes.at[group, me],
            send_sem=code_send,
            recv_sem=code_recv.at[z],
            device_id=peer_of(d),
            device_id_type=MESH,
        ).start()

    own = pltpu.make_async_copy(grads_hbm.at[me], held.at[group, me], self_sem)
    own.start()
    codes[group, me] = codes_ref[me]

    def near(i, carry):
        send(z * PLANE + (w + i) % PLANE)
        return carry

    lax.fori_loop(1, PLANE, near, 0)
    rels = []
    for far in range(planes // 2, 0, -1):
        rels.append([far] if 2 * far == planes else [far, planes - far])
    for pair in rels:

        def farther(i, carry):
            for rel in pair:
                send(((z + rel) % planes) * PLANE + (w + i) % PLANE)
            return carry

        lax.fori_loop(0, PLANE, farther, 0)
    own.wait()

    def chunk(ref, g, zs, count=PLANE):
        return ref.at[g, pl.ds(zs * PLANE, count)]

    def pass_on(zs):
        return (
            pltpu.make_async_remote_copy(
                src_ref=chunk(held, group, zs),
                dst_ref=chunk(held, group, zs),
                send_sem=pass_send,
                recv_sem=pass_recv.at[zs],
                device_id=partner,
                device_id_type=MESH,
            ),
            pltpu.make_async_remote_copy(
                src_ref=chunk(codes, group, zs),
                dst_ref=chunk(codes, group, zs),
                send_sem=passc_send,
                recv_sem=passc_recv.at[zs],
                device_id=partner,
                device_id_type=MESH,
            ),
        )

    def take(rel):
        zs = (z + rel) % planes
        if rel == 0:
            lands = held.at[group, pl.ds(0, PLANE - 1)]
            landc = codes.at[group, pl.ds(0, PLANE - 1)]
        else:
            lands, landc = chunk(held, group, zs), chunk(codes, group, zs)
        pltpu.make_async_copy(lands, lands, grad_recv.at[zs]).wait()
        pltpu.make_async_copy(landc, landc, code_recv.at[zs]).wait()
        for copy in pass_on(zs):
            copy.start()

    slots = staged.shape[1]
    rows = PLANE * slots
    width = staged.shape[2]
    touch_count = sums_ref.shape[0]
    ones = jnp.ones((width, width), jnp.bfloat16)

    def add(rel, first):
        zs = (z + rel) % planes
        other = 1 - group
        lands, landc = chunk(held, other, zs), chunk(codes, other, zs)
        pltpu.make_async_copy(lands, lands, pass_recv.at[zs]).wait()
        pltpu.make_async_copy(landc, landc, passc_recv.at[zs]).wait()
        grads, blocks, offsets = [], [], []
        lane = lax.broadcasted_iota(jnp.int32, (rows, width), 1)
        slot = lax.broadcasted_iota(jnp.int32, (rows, width), 0) % slots
        for g in range(2):
            grads.append(held[g, pl.ds(zs * PLANE, PLANE)].reshape(rows, width))
            code = jnp.broadcast_to(
                codes[g, pl.ds(zs * PLANE, PLANE)], (PLANE, slots, width)
            ).reshape(rows, width)
            block = jnp.where(lane == slot, code >> 8, 0).astype(jnp.float32)
            offset = jnp.where(lane == slot, code & (BLOCK - 1), 0).astype(jnp.float32)
            blocks.append(block.astype(jnp.bfloat16))
            offsets.append(offset.astype(jnp.bfloat16))
        values = jnp.concatenate(grads, axis=0)
        block = jnp.dot(
            jnp.concatenate(blocks, axis=0), ones, preferred_element_type=jnp.float32
        ).astype(jnp.bfloat16)
        offset = lax.dot_general(
            ones[:16],
            jnp.concatenate(offsets, axis=0),
            (((1,), (1,)), ((), ())),
            preferred_element_type=jnp.float32,
        )
        target = lax.broadcasted_iota(jnp.int32, (BLOCK, 2 * rows), 0).astype(jnp.float32)
        onehot = jnp.where(jnp.broadcast_to(offset[:1], target.shape) == target, 1.0, 0.0)
        onehot = onehot.astype(jnp.bfloat16)
        for pair in range(touch_count // 2):
            picked = []
            for t in (2 * pair, 2 * pair + 1):
                wanted = touched_ref[0, t].astype(jnp.float32).astype(jnp.bfloat16)
                picked.append(jnp.where(block == wanted, values, jnp.bfloat16(0)))
            part = jnp.dot(
                onehot, jnp.concatenate(picked, axis=1), preferred_element_type=jnp.float32
            )
            for k in range(2):
                piece = part[:, k * width : (k + 1) * width]
                if first:
                    sums_ref[2 * pair + k] = piece
                else:
                    sums_ref[2 * pair + k] += piece

    order = [0]
    for pair in rels:
        order += pair
    take(order[0])
    for i, rel in enumerate(order):
        if i + 1 < planes:
            take(order[i + 1])
        add(rel, i == 0)

    def square(t, acc):
        v = sums_ref[t]
        return acc + jnp.sum((v * v).reshape(BLOCK // 8, 8, width), axis=0)

    part = lax.fori_loop(0, touch_count, square, jnp.zeros((8, width), jnp.float32))
    red[me] = jnp.sum(part, axis=0, keepdims=True)

    def tell(i, carry):
        d = (me + i) % shards
        pltpu.make_async_remote_copy(
            src_ref=red.at[me],
            dst_ref=red.at[me],
            send_sem=red_send,
            recv_sem=red_recv,
            device_id=peer_of(d),
            device_id_type=MESH,
        ).start()
        return carry

    lax.fori_loop(1, shards, tell, 0)
    rest = red.at[pl.ds(0, shards - 1)]
    pltpu.make_async_copy(rest, rest, red_recv).wait()
    total = jnp.sum(jnp.sum(red[...], axis=0), axis=1, keepdims=True)
    clip = clip_limit / jnp.maximum(jnp.sqrt(total), clip_limit)
    clip_ref[...] = jnp.broadcast_to(clip, clip_ref.shape)

    pltpu.make_async_copy(rest, rest, red_send).wait()
    sent = staged.at[pl.ds(0, shards - 1)]
    pltpu.make_async_copy(sent, sent, grad_send).wait()
    sentc = codes.at[0, pl.ds(0, shards - 1)]
    pltpu.make_async_copy(sentc, sentc, code_send).wait()
    pltpu.make_async_copy(held.at[0], held.at[0], pass_send).wait()
    pltpu.make_async_copy(codes.at[0], codes.at[0], passc_send).wait()


def update_kernel(per_step, touched_ref, sums_ref, clip_ref, table_ref, accum_ref, out_ref, next_ref, place):
    step = pl.program_id(0)
    touch_count = sums_ref.shape[0]
    width = sums_ref.shape[2]
    halves = BLOCK // width

    @pl.when(step == 0)
    def _():
        for b in range(place.shape[0]):
            place[b] = -1
        for t in range(touch_count):
            place[touched_ref[0, t]] = t

    clip = clip_ref[...]
    diagonal = lax.broadcasted_iota(jnp.int32, (width, width), 0) == lax.broadcasted_iota(
        jnp.int32, (width, width), 1
    )
    for j in range(per_step):
        where = place[step * per_step + j]
        span = pl.ds(j * BLOCK, BLOCK)

        @pl.when(where < 0)
        def _():
            out_ref[span, :] = table_ref[span, :]
            next_ref[j] = accum_ref[j]

        @pl.when(where >= 0)
        def _():
            for h in range(halves):
                part = pl.ds(h * width, width)
                rows = pl.ds(j * BLOCK + h * width, width)
                scaled = sums_ref[where, part, :] * clip
                mean = jnp.sum(scaled * scaled, axis=1, keepdims=True) * (1.0 / width)
                old = accum_ref[j, h : h + 1, :]
                column = jnp.sum(
                    jnp.where(diagonal, jnp.broadcast_to(old, (width, width)), 0.0),
                    axis=1,
                    keepdims=True,
                )
                out_ref[rows, :] = table_ref[rows, :] * (1.0 - DECAY_RATE) - LEARN_RATE * (
                    scaled / jnp.sqrt(column + mean)
                )
                next_ref[j, h : h + 1, :] = old + jnp.sum(
                    jnp.where(diagonal, jnp.broadcast_to(mean, (width, width)), 0.0),
                    axis=0,
                    keepdims=True,
                )


def body(row_ids, grad_rows, touched, block_home, embed_table, row_accum):
    shards, slots, width = grad_rows.shape[2:]
    table_rows = embed_table.shape[0]
    blocks_here = table_rows // BLOCK
    touch_count = touched.shape[1]
    vmem = pl.BlockSpec(memory_space=pltpu.VMEM)
    smem = pl.BlockSpec(memory_space=pltpu.SMEM)

    codes = pl.pallas_call(
        functools.partial(key_kernel, blocks_here),
        out_shape=jax.ShapeDtypeStruct((shards, 128), jnp.int32),
        in_specs=[vmem, vmem],
        out_specs=vmem,
    )(row_ids.reshape(shards, slots).T, block_home.reshape(-1, 128))

    clip_limit = CLIP_RMS * math.sqrt(shards * touch_count * BLOCK * width)
    dma = pltpu.SemaphoreType.DMA
    planes = shards // PLANE
    sums, clip = pl.pallas_call(
        functools.partial(exchange_kernel, clip_limit),
        out_shape=(
            jax.ShapeDtypeStruct((touch_count, BLOCK, width), jnp.float32),
            jax.ShapeDtypeStruct((1, width), jnp.float32),
        ),
        in_specs=[pl.BlockSpec(memory_space=pl.ANY), vmem, smem],
        out_specs=(vmem, vmem),
        scratch_shapes=[
            pltpu.VMEM((shards, slots, width), jnp.bfloat16),
            pltpu.VMEM((2, shards, slots, width), jnp.bfloat16),
            pltpu.VMEM((2, shards, 1, 128), jnp.int32),
            pltpu.VMEM((shards, 1, width), jnp.float32),
            dma,
            dma,
            dma,
            dma((planes,)),
            dma,
            dma((planes,)),
            dma,
            dma((planes,)),
            dma,
            dma((planes,)),
            dma,
            dma,
        ],
        compiler_params=pltpu.CompilerParams(
            collective_id=0, has_side_effects=True, vmem_limit_bytes=32 * 1024 * 1024
        ),
    )(grad_rows.reshape(shards, slots, width), codes.reshape(shards, 1, 128), touched)

    per_step = 5
    steps = blocks_here // per_step
    halves = BLOCK // width
    table, accum = pl.pallas_call(
        functools.partial(update_kernel, per_step),
        grid=(steps,),
        out_shape=(
            jax.ShapeDtypeStruct(embed_table.shape, jnp.float32),
            jax.ShapeDtypeStruct((blocks_here, halves, width), jnp.float32),
        ),
        in_specs=[
            smem,
            vmem,
            vmem,
            pl.BlockSpec((per_step * BLOCK, width), lambda i: (i, 0)),
            pl.BlockSpec((per_step, halves, width), lambda i: (i, 0, 0)),
        ],
        out_specs=(
            pl.BlockSpec((per_step * BLOCK, width), lambda i: (i, 0)),
            pl.BlockSpec((per_step, halves, width), lambda i: (i, 0, 0)),
        ),
        scratch_shapes=[pltpu.SMEM((blocks_here,), jnp.int32)],
        compiler_params=pltpu.CompilerParams(vmem_limit_bytes=24 * 1024 * 1024),
    )(touched, sums, clip, embed_table, row_accum.reshape(blocks_here, halves, width))
    return table, accum.reshape(-1)


def solution(mesh):
    placed = (
        P("rep", "shard", None, None),
        P("rep", "shard", None, None, None),
        P("shard", None),
        P(),
        P("shard", None),
        P("shard"),
    )
    return jax.shard_map(
        body, mesh=mesh, in_specs=placed, out_specs=(P("shard", None), P("shard")), check_vma=False
    )
```

time: 218 us -> 69.4 us (0.32)
  Pallas kernels: 0 us -> 62.6 us
  local copies, waits for them, and re-layouts: 55.4 us -> 5.79 us
  blocking collectives: 41.2 us -> 0 us
  matrix products: 39.7 us -> 0 us
  starting transfers between devices: 31.4 us -> 0 us
  waiting for transfers between devices: 26.7 us -> 0 us
  loops' own time: 13.5 us -> 0 us
  other arithmetic: 6.65 us -> 0 us
    pallas_call x0 -> x3, Pallas kernels: none -> 62.6 us  [the longest x1 54.2 us: body(): pl.pallas_call(functools.partial(exchange_kernel, clip_limit), out_shape=...]
    psum x4 -> x0, blocking collectives: 41.2 us -> none  [over_axes(): return functools.reduce(lax.psum, axes, x)]
    dot_general x20 -> x0, matrix products: 39.7 us -> none  [single_block(): return jnp.dot(onehot, gradients, preferred_element_type=jnp.float32)]
    all_to_all x4 -> x0, starting transfers between devices: 31.4 us -> none  [the longest x1 16.4 us: body(): lax.all_to_all(row_ids, SHARD, split_axis=2, concat_axis=2, tiled=True)]
    gather x3 -> x0, local copies, waits for them, and re-layouts: 28.3 us -> none  [the longest x1 23 us: slot_blocks(): local_block = block_home[safe_ids // BLOCK] % blocks_here]
    all_to_all x4 -> x0, waiting for transfers between devices: 26.7 us -> none  [the longest x2 15 us: sent_to_all(): return lax.all_to_all(copies, axis, split_axis=0, concat_axis=0, tiled=True)]
    another operation x1 -> x0, loops' own time: 13.5 us -> none  [block_sums(): return lax.map(single_block, jnp.arange(touch_count, dtype=jnp.int32))]
    dynamic_slice x20 -> x0, local copies, waits for them, and re-layouts: 11.7 us -> none  [block_sums(): return lax.map(single_block, jnp.arange(touch_count, dtype=jnp.int32))]
  transfers between devices with their start and end apart: 4 -> 0, of which waited for: 3 -> 0; matrix products, arithmetic and copies ran while one was open for 11% -> 0% of each run, Pallas kernels for 0% -> 0%
where the time goes in v1:
time: 69.4 us; the launch traced here: 69 us
  Pallas kernels  62.6 us (90%)
  local copies, waits for them, and re-layouts  5.79 us (8%)
    pallas_call x1, Pallas kernels, body(): pl.pallas_call(functools.partial(exchange_kernel, clip_limit), out_shape=...  54.2 us
    pallas_call x1, Pallas kernels, body(): pl.pallas_call(functools.partial(update_kernel, per_step), grid=(steps,),...  6.68 us
    unnamed x10, local copies, waits for them, and re-layouts  5.79 us
    pallas_call x1, Pallas kernels, body(): pl.pallas_call(functools.partial(key_kernel, blocks_here), out_shape=jax....  1.68 us

profile of v1, /device:TPU:1, one launch (start us, length us, event | category | flops | bytes accessed | tf_op | source)
XLA Modules:
  0.0 69.0 jit_solution(6474483465724303476)
XLA Ops:
  0.6 1.7 %shard_map.77 = s32[128,128]{1,0:T(8,128)} custom-call(s32[16,128]{1,0:T(8,128)} %bitcast.12, s32[40,128]{1,0:T(8,128)} %bitcast.11), custom_call_target="tpu_custom_call" | custom-call | tf_op jit(solution)/shard_map/pallas_call | solution.py:314
  2.3 0.0 copy-start.1
  2.3 1.0 %copy-done.1 = bf16[1,1,128,16,128]{4,3,2,1,0:T(8,128)(2,1)S(1)} copy-done((bf16[1,1,128,16,128]{4,3,2,1,0:T(8,128)(2,1)S(1)}, bf16[1,1,128,16,128]{4,3,2,1,0:T(8,128)(2,1)}, u32[]{:S(2)}) %copy-start.1) | copy-done | bytes 524312
  3.3 0.0 copy-start.2
  3.4 0.8 %copy-done.2 = s32[128,128]{1,0:T(8,128)S(1)} copy-done((s32[128,128]{1,0:T(8,128)S(1)}, s32[128,128]{1,0:T(8,128)}, u32[]{:S(2)}) %copy-start.2) | copy-done | bytes 65560
  4.2 0.0 copy-start.4
  4.2 0.7 copy-done.4
  4.8 54.2 %shard_map.78 = (f32[20,256,128]{2,1,0:T(8,128)S(1)}, f32[1,128]{1,0:T(1,128)S(1)}) custom-call(bf16[128,16,128]{2,1,0:T(8,128)(2,1)S(1)} %bitcast.8, s32[128,1,128]{2,1,0:T(1,128)S(1)} %bitcast.9, s32[1,20]{1,0:T(1,128)S(1)} %copy-done.4), custom_call_target="tpu_custom_call" | custom-call | tf_op jit(solution)/shard_map/pallas_call | solution.py:324
  59.1 0.0 copy-start
  59.1 2.5 %copy-done = f32[10240,128]{1,0:T(8,128)S(1)} copy-done((f32[10240,128]{1,0:T(8,128)S(1)}, f32[10240,128]{1,0:T(8,128)}, u32[]{:S(2)}) %copy-start) | copy-done | bytes 5242904
  61.6 0.0 copy-start.3
  61.6 0.8 %copy-done.3 = f32[10240]{0:T(1024)S(1)} copy-done((f32[10240]{0:T(1024)S(1)}, f32[10240]{0:T(1024)}, u32[]{:S(2)}) %copy-start.3) | copy-done | bytes 40984
  62.4 6.7 %shard_map.79 = (f32[10240,128]{1,0:T(8,128)}, f32[40,2,128]{2,1,0:T(2,128)}) custom-call(s32[1,20]{1,0:T(1,128)S(1)} %copy-done.4, f32[20,256,128]{2,1,0:T(8,128)S(1)} %get-tuple-element.6.sums_ref, f32[1,128]{1,0:T(1,128)S(1)} %get-tuple-element.7.clip_ref, f32[10240,128]{1,0:T(8,128)S(1)} %copy-done, f32[40,2,128]{2,1,0:T(2,128)S(1)} %bitcast.10), custom_call_target="tpu_custom_call" | custom-call | tf_op jit(solution)/shard_map/pallas_call | solution.py:358
Async XLA Ops:
  2.3 1.0 %copy-start.1 = (bf16[1,1,128,16,128]{4,3,2,1,0:T(8,128)(2,1)S(1)}, bf16[1,1,128,16,128]{4,3,2,1,0:T(8,128)(2,1)}, u32[]{:S(2)}) copy-start(bf16[1,1,128,16,128]{4,3,2,1,0:T(8,128)(2,1)} %param.7) | copy-start | bytes 1572868
  3.3 0.8 %copy-start.2 = (s32[128,128]{1,0:T(8,128)S(1)}, s32[128,128]{1,0:T(8,128)}, u32[]{:S(2)}) copy-start(s32[128,128]{1,0:T(8,128)} %shard_map.77) | copy-start | bytes 196612
  4.2 0.7 copy-start.4
  59.1 2.5 %copy-start = (f32[10240,128]{1,0:T(8,128)S(1)}, f32[10240,128]{1,0:T(8,128)}, u32[]{:S(2)}) copy-start(f32[10240,128]{1,0:T(8,128)} %table_ref.1) | copy-start | bytes 15728644
  61.6 0.8 %copy-start.3 = (f32[10240]{0:T(1024)S(1)}, f32[10240]{0:T(1024)}, u32[]{:S(2)}) copy-start(f32[10240]{0:T(1024)} %param.11) | copy-start | bytes 122884

commit v2 on v0

v2 whole, which is shorter than its diff:
```python
import functools
import math

import jax
import jax.numpy as jnp
from jax import lax
from jax.experimental import pallas as pl
from jax.experimental.pallas import tpu as pltpu
from jax.sharding import PartitionSpec as P

MESH = pl.DeviceIdType.MESH
BLOCK = 256
PLANE = 16
CLIP_RMS = 0.25
LEARN_RATE = 0.1
DECAY_RATE = 0.05


def slot_codes(ids, home_ref, blocks_here, planes):
    slots, dests = ids.shape
    live = ids >= 0
    safe = jnp.where(live, ids, 0)
    logical = safe >> 8
    high, low = logical >> 7, logical & 127
    stored = jnp.zeros_like(ids)
    for h in range(home_ref.shape[0]):
        row = jnp.broadcast_to(home_ref[h : h + 1, :], ids.shape)
        stored = jnp.where(high == h, jnp.take_along_axis(row, low, axis=1), stored)
    owner = lax.broadcasted_iota(jnp.int32, ids.shape, 1)
    local = stored - owner * blocks_here
    code = jnp.where(live, local * BLOCK + (safe & (BLOCK - 1)), -1)
    turned = [code] + [pltpu.roll(code, dests - PLANE * p, 1) for p in range(1, planes)]
    return jnp.concatenate(turned, axis=0).T[:PLANE]


def by_plane(raw, planes):
    sources, lanes = raw.shape
    slots = lanes // planes
    per_row = lanes // slots
    turned = [raw] + [pltpu.roll(raw, slots * m, 1) for m in range(1, per_row)]
    part = lax.broadcasted_iota(jnp.int32, raw.shape, 1) // slots
    source = lax.broadcasted_iota(jnp.int32, raw.shape, 0) % per_row
    found = []
    for p in range(planes):
        picked = jnp.zeros_like(raw)
        for j in range(per_row):
            picked = jnp.where((part == j) & (source == j), turned[(j - p) % per_row], picked)
        found.append(jnp.sum(picked.reshape(sources // per_row, per_row, lanes), axis=1))
    return found


def exchange_kernel(
    clip_limit,
    blocks_here,
    grads_hbm,
    ids_hbm,
    home_hbm,
    touched_hbm,
    sums_ref,
    means_ref,
    clip_ref,
    staged,
    relay,
    held,
    mine,
    raw,
    packed,
    codes,
    ids_ref,
    home_ref,
    touched_ref,
    red_plane,
    red_column,
    load_sem,
    direct_send,
    direct_recv,
    spread_send,
    spread_recv,
    relay_send,
    relay_recv,
    column_send,
    column_recv,
    pass_send,
    pass_recv,
    code_send,
    code_recv,
    ccode_send,
    ccode_recv,
    pcode_send,
    pcode_recv,
    redp_send,
    redp_recv,
    redc_send,
    redc_recv,
):
    rep, me = lax.axis_index("rep"), lax.axis_index("shard")
    shards, slots, width = staged.shape
    planes = shards // PLANE
    z, w = me // PLANE, me % PLANE
    group = (rep + (w // 2) % 2) % 2
    other = 1 - group
    partner = (1 - rep, me)
    mates = [(w + i) % PLANE for i in range(PLANE)]
    mate_ids = [((group + (to // 2) % 2) % 2, z * PLANE + to) for to in mates]

    def ahead(rel):
        return (z + rel) % planes

    def behind(rel):
        return (z + planes - rel) % planes

    def at_column(to):
        return (rep, to * PLANE + w)

    def remote(src, dst, send, recv, device):
        return pltpu.make_async_remote_copy(
            src_ref=src, dst_ref=dst, send_sem=send, recv_sem=recv, device_id=device, device_id_type=MESH
        )

    def wait(ref, sem):
        pltpu.make_async_copy(ref, ref, sem).wait()

    def chunk(ref, g, zs, count=PLANE):
        return ref.at[g, pl.ds(zs * PLANE, count)]

    barrier = pltpu.get_barrier_semaphore()
    for rel in range(planes - 1, 0, -1):
        pl.semaphore_signal(barrier, inc=1, device_id=at_column(ahead(rel)), device_id_type=MESH)
    for i in range(1, PLANE):
        pl.semaphore_signal(barrier, inc=1, device_id=mate_ids[i], device_id_type=MESH)
    pl.semaphore_signal(barrier, inc=1, device_id=partner, device_id_type=MESH)

    loads = [
        pltpu.make_async_copy(ids_hbm, ids_ref, load_sem.at[0]),
        pltpu.make_async_copy(home_hbm, home_ref, load_sem.at[1]),
        pltpu.make_async_copy(grads_hbm, staged, load_sem.at[2]),
        pltpu.make_async_copy(touched_hbm, touched_ref, load_sem.at[3]),
    ]
    for load in loads:
        load.start()

    near = []
    for rel in range(1, planes // 2 - 1):
        near += [rel, planes - rel]
    far = [planes // 2 - 1, planes // 2 + 1, planes // 2]

    for rel in [0] + far:
        to = ahead(rel)
        src = grads_hbm.at[to * PLANE + w]
        dst = held.at[group, me] if rel == 0 else relay.at[to, w]
        pltpu.make_async_copy(src, dst, relay_recv.at[to]).start()

    loads[0].wait()
    loads[1].wait()
    mine[...] = slot_codes(ids_ref[...], home_ref, blocks_here, planes).reshape(mine.shape)
    raw[w] = mine[w]
    loads[2].wait()
    loads[3].wait()
    pl.semaphore_wait(barrier, PLANE + planes - 1)

    for rel in near:
        to = ahead(rel)
        remote(
            staged.at[pl.ds(to * PLANE, PLANE)], relay.at[z], direct_send, direct_recv.at[z], at_column(to)
        ).start()
    for i in range(1, PLANE):
        remote(mine.at[mates[i]], raw.at[w], code_send, code_recv, mate_ids[i]).start()
    for rel in [0] + far:
        to = ahead(rel)
        for i in range(1, PLANE):
            dst = held.at[group, me] if rel == 0 else relay.at[to, w]
            remote(staged.at[to * PLANE + mates[i]], dst, relay_send, relay_recv.at[to], mate_ids[i]).start()

    wait(raw.at[pl.ds(0, PLANE - 1)], code_recv)
    for p, rows in enumerate(by_plane(raw[...].reshape(PLANE, planes * slots), planes)):
        packed[p] = rows
    codes[group, z] = packed[z]
    for rel in near + far:
        to = ahead(rel)
        remote(packed.at[to], codes.at[group, z], ccode_send, ccode_recv, at_column(to)).start()

    def send_column(rel):
        to = ahead(rel)
        wait(relay.at[to], relay_recv.at[to])
        remote(
            relay.at[to], chunk(held, group, z), column_send, column_recv.at[z], at_column(to)
        ).start()

    def spread(rel):
        zs = behind(rel)
        wait(relay.at[zs], direct_recv.at[zs])
        place = held.at[group, zs * PLANE + w]
        for i in range(1, PLANE):
            remote(relay.at[zs, mates[i]], place, spread_send, spread_recv.at[zs], mate_ids[i]).start()
        held[group, zs * PLANE + w] = relay[zs, w]

    def take(rel):
        zs = behind(rel)
        if rel == 0:
            wait(chunk(held, group, zs), relay_recv.at[zs])
        elif rel in near:
            wait(chunk(held, group, 0, PLANE - 1), spread_recv.at[zs])
        else:
            wait(chunk(held, group, zs), column_recv.at[zs])
        remote(
            chunk(held, group, zs), chunk(held, group, zs), pass_send, pass_recv.at[zs], partner
        ).start()

    rows = PLANE * slots
    touch_count = sums_ref.shape[0]
    ones = jnp.ones((width, width), jnp.bfloat16)
    diagonal = lax.broadcasted_iota(jnp.int32, (width, width), 0) == lax.broadcasted_iota(
        jnp.int32, (width, width), 1
    )

    def add(rel, first):
        zs = behind(rel)
        wait(chunk(held, other, zs), pass_recv.at[zs])
        grads, blocks, offsets = [], [], []
        for g in range(2):
            grads.append(held[g, pl.ds(zs * PLANE, PLANE)].reshape(rows, width))
            code = codes[g, zs]
            for r in range(rows // width):
                line = code[r : r + 1]
                block = jnp.where(diagonal, jnp.broadcast_to(line >> 8, diagonal.shape), 0)
                blocks.append(block.astype(jnp.float32).astype(jnp.bfloat16))
                offsets.append(line & (BLOCK - 1))
        values = jnp.concatenate(grads, axis=0)
        block = jnp.dot(
            jnp.concatenate(blocks, axis=0), ones, preferred_element_type=jnp.float32
        ).astype(jnp.bfloat16)
        target = lax.broadcasted_iota(jnp.int32, (BLOCK, 2 * rows), 0)
        offset = jnp.broadcast_to(jnp.concatenate(offsets, axis=1), target.shape)
        onehot = jnp.where(offset == target, 1.0, 0.0).astype(jnp.bfloat16)
        for pair in range(touch_count // 2):
            picked = []
            for t in (2 * pair, 2 * pair + 1):
                wanted = touched_ref[0, t].astype(jnp.float32).astype(jnp.bfloat16)
                picked.append(jnp.where(block == wanted, values, jnp.bfloat16(0)))
            part = jnp.dot(
                onehot, jnp.concatenate(picked, axis=1), preferred_element_type=jnp.float32
            )
            for k in range(2):
                piece = part[:, k * width : (k + 1) * width]
                if first:
                    sums_ref[2 * pair + k] = piece
                else:
                    sums_ref[2 * pair + k] += piece

    for rel in far:
        send_column(rel)
    take(0)
    for rel in near:
        spread(rel)
    wait(codes.at[group, pl.ds(0, planes - 1)], ccode_recv)
    remote(codes.at[group], codes.at[group], pcode_send, pcode_recv, partner).start()
    every = [0] + near + far
    take(every[1])
    take(every[2])
    wait(codes.at[other], pcode_recv)
    for i, rel in enumerate(every):
        if i + 3 < planes:
            take(every[i + 3])
        add(rel, i == 0)

    def square(t, acc):
        v = sums_ref[t]
        return acc + jnp.sum((v * v).reshape(BLOCK // 8, 8, width), axis=0)

    part = lax.fori_loop(0, touch_count, square, jnp.zeros((8, width), jnp.float32))
    red_plane[w] = jnp.sum(part, axis=0, keepdims=True)
    for i in range(1, PLANE):
        remote(red_plane.at[w], red_plane.at[w], redp_send, redp_recv, mate_ids[i]).start()

    def row_means(t, carry):
        for h in range(BLOCK // width):
            v = sums_ref[t, pl.ds(h * width, width), :]
            mean = jnp.sum(v * v, axis=1, keepdims=True) * (1.0 / width)
            means_ref[t, h : h + 1, :] = jnp.sum(
                jnp.where(diagonal, jnp.broadcast_to(mean, diagonal.shape), 0.0), axis=0, keepdims=True
            )
        return carry

    lax.fori_loop(0, touch_count, row_means, 0)

    wait(red_plane.at[pl.ds(0, PLANE - 1)], redp_recv)
    red_column[z] = jnp.sum(red_plane[...], axis=0)
    for rel in range(1, planes):
        remote(red_column.at[z], red_column.at[z], redc_send, redc_recv, at_column(ahead(rel))).start()
    wait(red_column.at[pl.ds(0, planes - 1)], redc_recv)
    total = jnp.sum(jnp.sum(red_column[...], axis=0), axis=1, keepdims=True)
    clip = clip_limit / jnp.maximum(jnp.sqrt(total), clip_limit)
    clip_ref[...] = jnp.broadcast_to(clip, clip_ref.shape)

    wait(red_plane.at[pl.ds(0, PLANE - 1)], redp_send)
    wait(red_column.at[pl.ds(0, planes - 1)], redc_send)
    wait(mine.at[pl.ds(0, PLANE - 1)], code_send)
    wait(packed.at[pl.ds(0, planes - 1)], ccode_send)
    wait(codes.at[0], pcode_send)
    wait(staged.at[pl.ds(0, len(near) * PLANE)], direct_send)
    wait(staged.at[pl.ds(0, len(near) * (PLANE - 1))], spread_send)
    wait(staged.at[pl.ds(0, (len(far) + 1) * (PLANE - 1))], relay_send)
    wait(staged.at[pl.ds(0, len(far) * PLANE)], column_send)
    wait(held.at[0], pass_send)


def update_kernel(
    touched_ref,
    sums_ref,
    means_ref,
    clip_ref,
    table_ref,
    accum_ref,
    out_ref,
    next_ref,
    place,
    fresh,
    following,
    kept_sem,
    fresh_sem,
    next_sem,
):
    touch_count, _, width = sums_ref.shape
    blocks_here = table_ref.shape[0]
    halves = BLOCK // width

    for b in range(blocks_here):
        place[b] = 0
    for t in range(touch_count):
        place[touched_ref[0, t]] = 1
    for b in range(blocks_here):

        @pl.when(place[b] == 0)
        def _():
            pltpu.make_async_copy(table_ref.at[b], out_ref.at[b], kept_sem).start()

    clip = clip_ref[...]
    following[...] = accum_ref[...]
    for t in range(touch_count):
        b = touched_ref[0, t]
        following[b] = accum_ref[b] + clip * clip * means_ref[t]
    done = pltpu.make_async_copy(following, next_ref, next_sem)
    done.start()

    diagonal = lax.broadcasted_iota(jnp.int32, (width, width), 0) == lax.broadcasted_iota(
        jnp.int32, (width, width), 1
    )

    def renew(t, carry):
        b = touched_ref[0, t]
        rate = (LEARN_RATE * clip) / jnp.sqrt(following[b])
        for h in range(halves):
            column = jnp.sum(
                jnp.where(diagonal, jnp.broadcast_to(rate[h : h + 1], diagonal.shape), 0.0),
                axis=1,
                keepdims=True,
            )
            part = pl.ds(h * width, width)
            fresh[t, part, :] = table_ref[b, part, :] * (1.0 - DECAY_RATE) - column * sums_ref[t, part, :]
        pltpu.make_async_copy(fresh.at[t], out_ref.at[b], fresh_sem).start()
        return carry

    lax.fori_loop(0, touch_count, renew, 0)
    kept = table_ref.at[pl.ds(0, blocks_here - touch_count)]
    pltpu.make_async_copy(kept, kept, kept_sem).wait()
    pltpu.make_async_copy(fresh, fresh, fresh_sem).wait()
    done.wait()


def body(row_ids, grad_rows, touched, block_home, embed_table, row_accum):
    shards, slots, width = grad_rows.shape[2:]
    blocks_here = embed_table.shape[0] // BLOCK
    touch_count = touched.shape[1]
    halves = BLOCK // width
    planes = shards // PLANE
    vmem = pl.BlockSpec(memory_space=pltpu.VMEM)
    smem = pl.BlockSpec(memory_space=pltpu.SMEM)
    hbm = pl.BlockSpec(memory_space=pltpu.HBM)
    dma = pltpu.SemaphoreType.DMA
    f32 = jnp.float32

    clip_limit = CLIP_RMS * math.sqrt(shards * touch_count * BLOCK * width)
    homes = block_home.reshape(-1, 128)
    sums, means, clip = pl.pallas_call(
        functools.partial(exchange_kernel, clip_limit, blocks_here),
        out_shape=(
            jax.ShapeDtypeStruct((touch_count, BLOCK, width), f32),
            jax.ShapeDtypeStruct((touch_count, halves, width), f32),
            jax.ShapeDtypeStruct((1, width), f32),
        ),
        in_specs=[hbm] * 4,
        out_specs=(vmem, vmem, vmem),
        scratch_shapes=[
            pltpu.VMEM((shards, slots, width), jnp.bfloat16),
            pltpu.VMEM((planes, PLANE, slots, width), jnp.bfloat16),
            pltpu.VMEM((2, shards, slots, width), jnp.bfloat16),
            pltpu.VMEM((PLANE, 1, 128), jnp.int32),
            pltpu.VMEM((PLANE, 1, 128), jnp.int32),
            pltpu.VMEM((planes, PLANE * slots // 128, 128), jnp.int32),
            pltpu.VMEM((2, planes, PLANE * slots // 128, 128), jnp.int32),
            pltpu.VMEM((slots, shards), jnp.int32),
            pltpu.VMEM(homes.shape, jnp.int32),
            pltpu.SMEM(touched.shape, jnp.int32),
            pltpu.VMEM((PLANE, 1, width), f32),
            pltpu.VMEM((planes, 1, width), f32),
            dma((4,)),
            dma,
            dma((planes,)),
            dma,
            dma((planes,)),
            dma,
            dma((planes,)),
            dma,
            dma((planes,)),
            dma,
            dma((planes,)),
            *([dma] * 10),
        ],
        compiler_params=pltpu.CompilerParams(
            collective_id=0, has_side_effects=True, vmem_limit_bytes=24 * 1024 * 1024
        ),
        cost_estimate=pl.CostEstimate(
            flops=4 * shards * slots * touch_count * BLOCK * width,
            bytes_accessed=2 * shards * slots * width,
            transcendentals=0,
        ),
    )(
        *(
            pltpu.with_memory_space_constraint(x, pltpu.HBM)
            for x in (
                grad_rows.reshape(shards, slots, width),
                row_ids.reshape(shards, slots).T,
                homes,
                touched,
            )
        )
    )

    table, accum = pl.pallas_call(
        update_kernel,
        out_shape=(
            jax.ShapeDtypeStruct((blocks_here, BLOCK, width), f32),
            jax.ShapeDtypeStruct((blocks_here, halves, width), f32),
        ),
        in_specs=[smem, vmem, vmem, vmem, vmem, vmem],
        out_specs=(hbm, hbm),
        scratch_shapes=[
            pltpu.SMEM((blocks_here,), jnp.int32),
            pltpu.VMEM((touch_count, BLOCK, width), f32),
            pltpu.VMEM((blocks_here, halves, width), f32),
            dma,
            dma,
            dma,
        ],
        compiler_params=pltpu.CompilerParams(vmem_limit_bytes=24 * 1024 * 1024),
    )(
        touched,
        sums,
        means,
        clip,
        embed_table.reshape(blocks_here, BLOCK, width),
        row_accum.reshape(blocks_here, halves, width),
    )
    return table.reshape(embed_table.shape), accum.reshape(-1)


def solution(mesh):
    placed = (
        P("rep", "shard", None, None),
        P("rep", "shard", None, None, None),
        P("shard", None),
        P(),
        P("shard", None),
        P("shard"),
    )
    return jax.shard_map(
        body, mesh=mesh, in_specs=placed, out_specs=(P("shard", None), P("shard")), check_vma=False
    )
```

time: 218 us -> 47.5 us (0.22)
  local copies, waits for them, and re-layouts: 55.4 us -> 0.01 us
  Pallas kernels: 0 us -> 46.6 us
  blocking collectives: 41.2 us -> 0 us
  matrix products: 39.7 us -> 0 us
  starting transfers between devices: 31.4 us -> 0 us
  waiting for transfers between devices: 26.7 us -> 0 us
  loops' own time: 13.5 us -> 0 us
  other arithmetic: 6.65 us -> 0 us
    pallas_call x0 -> x2, Pallas kernels: none -> 46.6 us  [the longest x1 42.6 us: body(): pl.pallas_call(functools.partial(exchange_kernel, clip_limit, blocks_here...]
    psum x4 -> x0, blocking collectives: 41.2 us -> none  [over_axes(): return functools.reduce(lax.psum, axes, x)]
    dot_general x20 -> x0, matrix products: 39.7 us -> none  [single_block(): return jnp.dot(onehot, gradients, preferred_element_type=jnp.float32)]
    all_to_all x4 -> x0, starting transfers between devices: 31.4 us -> none  [the longest x1 16.4 us: body(): lax.all_to_all(row_ids, SHARD, split_axis=2, concat_axis=2, tiled=True)]
    gather x3 -> x0, local copies, waits for them, and re-layouts: 28.3 us -> none  [the longest x1 23 us: slot_blocks(): local_block = block_home[safe_ids // BLOCK] % blocks_here]
    all_to_all x4 -> x0, waiting for transfers between devices: 26.7 us -> none  [the longest x2 15 us: sent_to_all(): return lax.all_to_all(copies, axis, split_axis=0, concat_axis=0, tiled=True)]
    another operation x1 -> x0, loops' own time: 13.5 us -> none  [block_sums(): return lax.map(single_block, jnp.arange(touch_count, dtype=jnp.int32))]
    dynamic_slice x20 -> x0, local copies, waits for them, and re-layouts: 11.7 us -> none  [block_sums(): return lax.map(single_block, jnp.arange(touch_count, dtype=jnp.int32))]
  transfers between devices with their start and end apart: 4 -> 0, of which waited for: 3 -> 0; matrix products, arithmetic and copies ran while one was open for 11% -> 0% of each run, Pallas kernels for 0% -> 0%
where the time goes in v2:
time: 47.5 us; the launch traced here: 47.3 us
  Pallas kernels  46.6 us (98%)
  between operations  0.69 us (1%)
    pallas_call x1, Pallas kernels, body(): pl.pallas_call(functools.partial(exchange_kernel, clip_limit, blocks_here...  42.6 us
    pallas_call x1, Pallas kernels, body(): pl.pallas_call(update_kernel, out_shape=(jax.ShapeDtypeStruct((blocks_her...  3.93 us

profile of v2, /device:TPU:1, one launch (start us, length us, event | category | flops | bytes accessed | tf_op | source)
XLA Modules:
  0.0 47.3 jit_solution(14476214378595330656)
XLA Ops:
  0.6 0.0 copy-start
  0.6 0.0 copy-start.1
  0.7 0.0 copy-start.2
  0.7 42.6 %shard_map.77 = (f32[20,256,128]{2,1,0:T(8,128)S(1)}, f32[20,2,128]{2,1,0:T(2,128)S(1)}, f32[1,128]{1,0:T(1,128)S(1)}) custom-call(bf16[128,16,128]{2,1,0:T(8,128)(2,1)} %bitcast.12, s32[16,128]{1,0:T(8,128)} %bitcast.15, s32[40,128]{1,0:T(8,128)} %bitcast.14, s32[1,20]{1,0:T(1,128)} %touched_ref.1), custom_call_target="tpu_custom_call" | custom-call | flops 5368709120 | bytes 524288 | tf_op jit(solution)/shard_map/pallas_call | solution.py:384
  43.3 0.0 copy-done
  43.3 0.0 copy-done.1
  43.3 0.0 copy-done.2
  43.3 3.9 %shard_map.78 = (f32[40,256,128]{2,1,0:T(8,128)}, f32[40,2,128]{2,1,0:T(2,128)}) custom-call(s32[1,20]{1,0:T(1,128)S(1)} %copy-done.2, f32[20,256,128]{2,1,0:T(8,128)S(1)} %get-tuple-element.7.sums_ref, f32[20,2,128]{2,1,0:T(2,128)S(1)} %get-tuple-element.8.means_ref, f32[1,128]{1,0:T(1,128)S(1)} %get-tuple-element.9.clip_ref, f32[40,256,128]{2,1,0:T(8,128)S(1)} %bitcast.9, ...), custom_call_target="tpu_custom_call" | custom-call | tf_op jit(solution)/shard_map/pallas_call | solution.py:439
Async XLA Ops:
  0.6 42.7 %copy-start = (f32[10240,128]{1,0:T(8,128)S(1)}, f32[10240,128]{1,0:T(8,128)}, u32[]{:S(2)}) copy-start(f32[10240,128]{1,0:T(8,128)} %param.10) | copy-start | bytes 15728644
  0.6 42.7 %copy-start.1 = (f32[10240]{0:T(1024)S(1)}, f32[10240]{0:T(1024)}, u32[]{:S(2)}) copy-start(f32[10240]{0:T(1024)} %param.11) | copy-start | bytes 122884
  0.7 42.7 %copy-start.2 = (s32[1,20]{1,0:T(1,128)S(1)}, s32[1,20]{1,0:T(1,128)}, u32[]{:S(2)}) copy-start(s32[1,20]{1,0:T(1,128)} %touched_ref.1) | copy-start | bytes 244

commit v3 on v2

--- a/solution.py
+++ b/solution.py
@@ -72,6 +72,7 @@
     red_plane,
     red_column,
     load_sem,
+    beyond_sem,
     direct_send,
     direct_recv,
     spread_send,
@@ -123,8 +124,13 @@
     def chunk(ref, g, zs, count=PLANE):
         return ref.at[g, pl.ds(zs * PLANE, count)]
 
+    near = []
+    for rel in range(1, planes // 2 - 1):
+        near += [rel, planes - rel]
+    far = [planes // 2 - 1, planes // 2 + 1, planes // 2]
+
     barrier = pltpu.get_barrier_semaphore()
-    for rel in range(planes - 1, 0, -1):
+    for rel in near[::-1]:
         pl.semaphore_signal(barrier, inc=1, device_id=at_column(ahead(rel)), device_id_type=MESH)
     for i in range(1, PLANE):
         pl.semaphore_signal(barrier, inc=1, device_id=mate_ids[i], device_id_type=MESH)
@@ -139,11 +145,6 @@
     for load in loads:
         load.start()
 
-    near = []
-    for rel in range(1, planes // 2 - 1):
-        near += [rel, planes - rel]
-    far = [planes // 2 - 1, planes // 2 + 1, planes // 2]
-
     for rel in [0] + far:
         to = ahead(rel)
         src = grads_hbm.at[to * PLANE + w]
@@ -156,35 +157,57 @@
     raw[w] = mine[w]
     loads[2].wait()
     loads[3].wait()
-    pl.semaphore_wait(barrier, PLANE + planes - 1)
+    pl.semaphore_wait(barrier, PLANE + len(near))
+    for rel in near[2:]:
+        pl.semaphore_signal(beyond_sem, inc=1, device_id=at_column(ahead(rel)), device_id_type=MESH)
+
+    def send_codes():
+        for i in range(1, PLANE):
+            remote(mine.at[mates[i]], raw.at[w], code_send, code_recv, mate_ids[i]).start()
+
+    def send_mates(rel):
+        to = ahead(rel)
+        for i in range(1, PLANE):
+            dst = held.at[group, me] if rel == 0 else relay.at[to, w]
+            remote(staged.at[to * PLANE + mates[i]], dst, relay_send, relay_recv.at[to], mate_ids[i]).start()
 
     for rel in near:
         to = ahead(rel)
         remote(
             staged.at[pl.ds(to * PLANE, PLANE)], relay.at[z], direct_send, direct_recv.at[z], at_column(to)
         ).start()
-    for i in range(1, PLANE):
-        remote(mine.at[mates[i]], raw.at[w], code_send, code_recv, mate_ids[i]).start()
-    for rel in [0] + far:
-        to = ahead(rel)
-        for i in range(1, PLANE):
-            dst = held.at[group, me] if rel == 0 else relay.at[to, w]
-            remote(staged.at[to * PLANE + mates[i]], dst, relay_send, relay_recv.at[to], mate_ids[i]).start()
+    send_codes()
+    send_mates(0)
+    for rel in far:
+        send_mates(rel)
 
     wait(raw.at[pl.ds(0, PLANE - 1)], code_recv)
     for p, rows in enumerate(by_plane(raw[...].reshape(PLANE, planes * slots), planes)):
         packed[p] = rows
     codes[group, z] = packed[z]
+    pl.semaphore_wait(beyond_sem, 2)
     for rel in near + far:
         to = ahead(rel)
         remote(packed.at[to], codes.at[group, z], ccode_send, ccode_recv, at_column(to)).start()
 
+    half = PLANE // 2
+
     def send_column(rel):
         to = ahead(rel)
         wait(relay.at[to], relay_recv.at[to])
-        remote(
-            relay.at[to], chunk(held, group, z), column_send, column_recv.at[z], at_column(to)
-        ).start()
+        if rel != far[-1]:
+            remote(
+                relay.at[to], chunk(held, group, z), column_send, column_recv.at[0, z], at_column(to)
+            ).start()
+            return
+        for k in range(2):
+            remote(
+                relay.at[to, pl.ds(k * half, half)],
+                held.at[group, pl.ds(z * PLANE + k * half, half)],
+                column_send,
+                column_recv.at[k, z],
+                at_column(to),
+            ).start()
 
     def spread(rel):
         zs = behind(rel)
@@ -200,11 +223,20 @@
             wait(chunk(held, group, zs), relay_recv.at[zs])
         elif rel in near:
             wait(chunk(held, group, 0, PLANE - 1), spread_recv.at[zs])
-        else:
-            wait(chunk(held, group, zs), column_recv.at[zs])
-        remote(
-            chunk(held, group, zs), chunk(held, group, zs), pass_send, pass_recv.at[zs], partner
-        ).start()
+        if rel not in far:
+            remote(
+                chunk(held, group, zs), chunk(held, group, zs), pass_send, pass_recv.at[zs], partner
+            ).start()
+            return
+        if rel != far[-1]:
+            piece = chunk(held, group, zs)
+            wait(piece, column_recv.at[0, zs])
+            remote(piece, piece, pass_send, pass_recv.at[zs], partner).start()
+            return
+        for k in range(2):
+            piece = held.at[group, pl.ds(zs * PLANE + k * half, half)]
+            wait(piece, column_recv.at[k, zs])
+            remote(piece, piece, pass_send, pass_recv.at[zs], partner).start()
 
     rows = PLANE * slots
     touch_count = sums_ref.shape[0]
@@ -213,7 +245,7 @@
         jnp.int32, (width, width), 1
     )
 
-    def add(rel, first):
+    def add(rel, first, last, squares):
         zs = behind(rel)
         wait(chunk(held, other, zs), pass_recv.at[zs])
         grads, blocks, offsets = [], [], []
@@ -242,32 +274,30 @@
             )
             for k in range(2):
                 piece = part[:, k * width : (k + 1) * width]
-                if first:
-                    sums_ref[2 * pair + k] = piece
-                else:
-                    sums_ref[2 * pair + k] += piece
+                if not first:
+                    piece += sums_ref[2 * pair + k]
+                sums_ref[2 * pair + k] = piece
+                if last:
+                    squares += jnp.sum((piece * piece).reshape(BLOCK // 8, 8, width), axis=0)
+        return squares
 
     for rel in far:
         send_column(rel)
     take(0)
+    every = [0] + near + far
     for rel in near:
         spread(rel)
     wait(codes.at[group, pl.ds(0, planes - 1)], ccode_recv)
     remote(codes.at[group], codes.at[group], pcode_send, pcode_recv, partner).start()
-    every = [0] + near + far
     take(every[1])
     take(every[2])
     wait(codes.at[other], pcode_recv)
+    part = jnp.zeros((8, width), jnp.float32)
     for i, rel in enumerate(every):
         if i + 3 < planes:
             take(every[i + 3])
-        add(rel, i == 0)
-
-    def square(t, acc):
-        v = sums_ref[t]
-        return acc + jnp.sum((v * v).reshape(BLOCK // 8, 8, width), axis=0)
-
-    part = lax.fori_loop(0, touch_count, square, jnp.zeros((8, width), jnp.float32))
+        part = add(rel, i == 0, i + 1 == planes, part)
+
     red_plane[w] = jnp.sum(part, axis=0, keepdims=True)
     for i in range(1, PLANE):
         remote(red_plane.at[w], red_plane.at[w], redp_send, redp_recv, mate_ids[i]).start()
@@ -360,7 +390,7 @@
         pltpu.make_async_copy(fresh.at[t], out_ref.at[b], fresh_sem).start()
         return carry
 
-    lax.fori_loop(0, touch_count, renew, 0)
+    lax.fori_loop(0, touch_count, renew, 0, unroll=5)
     kept = table_ref.at[pl.ds(0, blocks_here - touch_count)]
     pltpu.make_async_copy(kept, kept, kept_sem).wait()
     pltpu.make_async_copy(fresh, fresh, fresh_sem).wait()
@@ -404,6 +434,7 @@
             pltpu.VMEM((PLANE, 1, width), f32),
             pltpu.VMEM((planes, 1, width), f32),
             dma((4,)),
+            pltpu.SemaphoreType.REGULAR,
             dma,
             dma((planes,)),
             dma,
@@ -411,7 +442,7 @@
             dma,
             dma((planes,)),
             dma,
-            dma((planes,)),
+            dma((2, planes)),
             dma,
             dma((planes,)),
             *([dma] * 10),

time: 47.5 us -> 45.8 us (0.964)
  Pallas kernels: 46.6 us -> 44.9 us
    pallas_call x1, Pallas kernels: 3.93 us -> 2.93 us  [body(): pl.pallas_call(update_kernel, out_shape=(jax.ShapeDtypeStruct((blocks_her...]
    pallas_call x1, Pallas kernels: 42.6 us -> 42 us  [body(): pl.pallas_call(functools.partial(exchange_kernel, clip_limit, blocks_here...]
where the time goes in v3:
time: 45.8 us; the launch traced here: 45.6 us
  Pallas kernels  44.9 us (98%)
  between operations  0.69 us (2%)
    pallas_call x1, Pallas kernels, body(): pl.pallas_call(functools.partial(exchange_kernel, clip_limit, blocks_here...  42 us
    pallas_call x1, Pallas kernels, body(): pl.pallas_call(update_kernel, out_shape=(jax.ShapeDtypeStruct((blocks_her...  2.93 us

profile of v3, /device:TPU:1, one launch (start us, length us, event | category | flops | bytes accessed | tf_op | source)
XLA Modules:
  0.0 45.6 jit_solution(1858337670923646509)
XLA Ops:
  0.6 0.0 copy-start
  0.6 0.0 copy-start.1
  0.7 0.0 copy-start.2
  0.7 42.0 %shard_map.77 = (f32[20,256,128]{2,1,0:T(8,128)S(1)}, f32[20,2,128]{2,1,0:T(2,128)S(1)}, f32[1,128]{1,0:T(1,128)S(1)}) custom-call(bf16[128,16,128]{2,1,0:T(8,128)(2,1)} %bitcast.12, s32[16,128]{1,0:T(8,128)} %bitcast.15, s32[40,128]{1,0:T(8,128)} %bitcast.14, s32[1,20]{1,0:T(1,128)} %touched_ref.1), custom_call_target="tpu_custom_call" | custom-call | flops 5368709120 | bytes 524288 | tf_op jit(solution)/shard_map/pallas_call | solution.py:414
  42.6 0.0 copy-done
  42.6 0.0 copy-done.1
  42.7 0.0 copy-done.2
  42.7 2.9 %shard_map.78 = (f32[40,256,128]{2,1,0:T(8,128)}, f32[40,2,128]{2,1,0:T(2,128)}) custom-call(s32[1,20]{1,0:T(1,128)S(1)} %copy-done.2, f32[20,256,128]{2,1,0:T(8,128)S(1)} %get-tuple-element.7.sums_ref, f32[20,2,128]{2,1,0:T(2,128)S(1)} %get-tuple-element.8.means_ref, f32[1,128]{1,0:T(1,128)S(1)} %get-tuple-element.9.clip_ref, f32[40,256,128]{2,1,0:T(8,128)S(1)} %bitcast.9, ...), custom_call_target="tpu_custom_call" | custom-call | tf_op jit(solution)/shard_map/pallas_call | solution.py:470
Async XLA Ops:
  0.6 42.0 %copy-start = (f32[10240,128]{1,0:T(8,128)S(1)}, f32[10240,128]{1,0:T(8,128)}, u32[]{:S(2)}) copy-start(f32[10240,128]{1,0:T(8,128)} %param.10) | copy-start | bytes 15728644
  0.6 42.0 %copy-start.1 = (f32[10240]{0:T(1024)S(1)}, f32[10240]{0:T(1024)}, u32[]{:S(2)}) copy-start(f32[10240]{0:T(1024)} %param.11) | copy-start | bytes 122884
  0.7 42.0 %copy-start.2 = (s32[1,20]{1,0:T(1,128)S(1)}, s32[1,20]{1,0:T(1,128)}, u32[]{:S(2)}) copy-start(s32[1,20]{1,0:T(1,128)} %touched_ref.1) | copy-start | bytes 244

commit v4 on v3

--- a/solution.py
+++ b/solution.py
@@ -224,9 +224,9 @@
         elif rel in near:
             wait(chunk(held, group, 0, PLANE - 1), spread_recv.at[zs])
         if rel not in far:
-            remote(
-                chunk(held, group, zs), chunk(held, group, zs), pass_send, pass_recv.at[zs], partner
-            ).start()
+            for k in range(4):
+                piece = held.at[group, pl.ds(zs * PLANE + k * (PLANE // 4), PLANE // 4)]
+                remote(piece, piece, pass_send, pass_recv.at[zs], partner).start()
             return
         if rel != far[-1]:
             piece = chunk(held, group, zs)
@@ -281,21 +281,22 @@
                     squares += jnp.sum((piece * piece).reshape(BLOCK // 8, 8, width), axis=0)
         return squares
 
-    for rel in far:
+    for rel in far[:-1]:
         send_column(rel)
     take(0)
     every = [0] + near + far
     for rel in near:
         spread(rel)
+    send_column(far[-1])
     wait(codes.at[group, pl.ds(0, planes - 1)], ccode_recv)
     remote(codes.at[group], codes.at[group], pcode_send, pcode_recv, partner).start()
-    take(every[1])
-    take(every[2])
+    for rel in every[1:5]:
+        take(rel)
     wait(codes.at[other], pcode_recv)
     part = jnp.zeros((8, width), jnp.float32)
     for i, rel in enumerate(every):
-        if i + 3 < planes:
-            take(every[i + 3])
+        if i + 5 < planes:
+            take(every[i + 5])
         part = add(rel, i == 0, i + 1 == planes, part)
 
     red_plane[w] = jnp.sum(part, axis=0, keepdims=True)

time: 45.8 us -> 45.8 us (level)
  no operation moved by 1% of the time
where the time goes in v4:
time: 45.8 us; the launch traced here: 45.7 us
  Pallas kernels  45 us (98%)
  between operations  0.69 us (2%)
    pallas_call x1, Pallas kernels, body(): pl.pallas_call(functools.partial(exchange_kernel, clip_limit, blocks_here...  42 us
    pallas_call x1, Pallas kernels, body(): pl.pallas_call(update_kernel, out_shape=(jax.ShapeDtypeStruct((blocks_her...  2.93 us

profile of v4, /device:TPU:1, one launch (start us, length us, event | category | flops | bytes accessed | tf_op | source)
XLA Modules:
  0.0 45.7 jit_solution(3298605021001210794)
XLA Ops:
  0.6 0.0 copy-start
  0.6 0.0 copy-start.1
  0.7 0.0 copy-start.2
  0.7 42.0 %shard_map.77 = (f32[20,256,128]{2,1,0:T(8,128)S(1)}, f32[20,2,128]{2,1,0:T(2,128)S(1)}, f32[1,128]{1,0:T(1,128)S(1)}) custom-call(bf16[128,16,128]{2,1,0:T(8,128)(2,1)} %bitcast.12, s32[16,128]{1,0:T(8,128)} %bitcast.15, s32[40,128]{1,0:T(8,128)} %bitcast.14, s32[1,20]{1,0:T(1,128)} %touched_ref.1), custom_call_target="tpu_custom_call" | custom-call | flops 5368709120 | bytes 524288 | tf_op jit(solution)/shard_map/pallas_call | solution.py:415
  42.7 0.0 copy-done
  42.7 0.0 copy-done.1
  42.7 0.0 copy-done.2
  42.7 2.9 %shard_map.78 = (f32[40,256,128]{2,1,0:T(8,128)}, f32[40,2,128]{2,1,0:T(2,128)}) custom-call(s32[1,20]{1,0:T(1,128)S(1)} %copy-done.2, f32[20,256,128]{2,1,0:T(8,128)S(1)} %get-tuple-element.7.sums_ref, f32[20,2,128]{2,1,0:T(2,128)S(1)} %get-tuple-element.8.means_ref, f32[1,128]{1,0:T(1,128)S(1)} %get-tuple-element.9.clip_ref, f32[40,256,128]{2,1,0:T(8,128)S(1)} %bitcast.9, ...), custom_call_target="tpu_custom_call" | custom-call | tf_op jit(solution)/shard_map/pallas_call | solution.py:471
Async XLA Ops:
  0.6 42.1 %copy-start = (f32[10240,128]{1,0:T(8,128)S(1)}, f32[10240,128]{1,0:T(8,128)}, u32[]{:S(2)}) copy-start(f32[10240,128]{1,0:T(8,128)} %param.10) | copy-start | bytes 15728644
  0.6 42.1 %copy-start.1 = (f32[10240]{0:T(1024)S(1)}, f32[10240]{0:T(1024)}, u32[]{:S(2)}) copy-start(f32[10240]{0:T(1024)} %param.11) | copy-start | bytes 122884
  0.7 42.1 %copy-start.2 = (s32[1,20]{1,0:T(1,128)S(1)}, s32[1,20]{1,0:T(1,128)}, u32[]{:S(2)}) copy-start(s32[1,20]{1,0:T(1,128)} %touched_ref.1) | copy-start | bytes 244

commit v5 on v4

--- a/solution.py
+++ b/solution.py
@@ -281,11 +281,13 @@
                     squares += jnp.sum((piece * piece).reshape(BLOCK // 8, 8, width), axis=0)
         return squares
 
+    take(0)
+    every = [0] + near + far
+    for rel in near[:2]:
+        spread(rel)
     for rel in far[:-1]:
         send_column(rel)
-    take(0)
-    every = [0] + near + far
-    for rel in near:
+    for rel in near[2:]:
         spread(rel)
     send_column(far[-1])
     wait(codes.at[group, pl.ds(0, planes - 1)], ccode_recv)

time: 45.8 us -> 45.8 us (level)
  no operation moved by 1% of the time
where the time goes in v5:
time: 45.8 us; the launch traced here: 45.7 us
  Pallas kernels  45 us (98%)
  between operations  0.69 us (2%)
    pallas_call x1, Pallas kernels, body(): pl.pallas_call(functools.partial(exchange_kernel, clip_limit, blocks_here...  42 us
    pallas_call x1, Pallas kernels, body(): pl.pallas_call(update_kernel, out_shape=(jax.ShapeDtypeStruct((blocks_her...  2.93 us

profile of v5, /device:TPU:1, one launch (start us, length us, event | category | flops | bytes accessed | tf_op | source)
XLA Modules:
  0.0 45.7 jit_solution(6204693619906343269)
XLA Ops:
  0.6 0.0 copy-start
  0.6 0.0 copy-start.1
  0.7 0.0 copy-start.2
  0.7 42.0 %shard_map.77 = (f32[20,256,128]{2,1,0:T(8,128)S(1)}, f32[20,2,128]{2,1,0:T(2,128)S(1)}, f32[1,128]{1,0:T(1,128)S(1)}) custom-call(bf16[128,16,128]{2,1,0:T(8,128)(2,1)} %bitcast.12, s32[16,128]{1,0:T(8,128)} %bitcast.15, s32[40,128]{1,0:T(8,128)} %bitcast.14, s32[1,20]{1,0:T(1,128)} %touched_ref.1), custom_call_target="tpu_custom_call" | custom-call | flops 5368709120 | bytes 524288 | tf_op jit(solution)/shard_map/pallas_call | solution.py:417
  42.7 0.0 copy-done
  42.7 0.0 copy-done.1
  42.7 0.0 copy-done.2
  42.7 2.9 %shard_map.78 = (f32[40,256,128]{2,1,0:T(8,128)}, f32[40,2,128]{2,1,0:T(2,128)}) custom-call(s32[1,20]{1,0:T(1,128)S(1)} %copy-done.2, f32[20,256,128]{2,1,0:T(8,128)S(1)} %get-tuple-element.7.sums_ref, f32[20,2,128]{2,1,0:T(2,128)S(1)} %get-tuple-element.8.means_ref, f32[1,128]{1,0:T(1,128)S(1)} %get-tuple-element.9.clip_ref, f32[40,256,128]{2,1,0:T(8,128)S(1)} %bitcast.9, ...), custom_call_target="tpu_custom_call" | custom-call | tf_op jit(solution)/shard_map/pallas_call | solution.py:473
Async XLA Ops:
  0.6 42.1 %copy-start = (f32[10240,128]{1,0:T(8,128)S(1)}, f32[10240,128]{1,0:T(8,128)}, u32[]{:S(2)}) copy-start(f32[10240,128]{1,0:T(8,128)} %param.10) | copy-start | bytes 15728644
  0.6 42.1 %copy-start.1 = (f32[10240]{0:T(1024)S(1)}, f32[10240]{0:T(1024)}, u32[]{:S(2)}) copy-start(f32[10240]{0:T(1024)} %param.11) | copy-start | bytes 122884
  0.7 42.1 %copy-start.2 = (s32[1,20]{1,0:T(1,128)S(1)}, s32[1,20]{1,0:T(1,128)}, u32[]{:S(2)}) copy-start(s32[1,20]{1,0:T(1,128)} %touched_ref.1) | copy-start | bytes 244
